TPU v7x, 256 devices: a whole 4x4x8 slice. The times are simulated.
256 devices in a mesh: seq: 64 (over y_lo, x, z), tensor: 4 (over y_hi, core).
Axes of the slice: x: 4, y: 4 (y_hi: 2, y_lo: 2; y = y_hi * 2 + y_lo), z: 8, core: 2. Of those that a mesh axis runs over, the one named last changes fastest.
Arguments:
- tokens: bfloat16 [32768, 2048], P('seq', 'tensor'), may hold values from -12 to 12
- attn_gain: float32 [2048], replicated, may hold values from 0.1 to 1.9
- w_query: bfloat16 [2048, 2048], P('seq', 'tensor'), as said below
- w_key: bfloat16 [2048, 512], P('seq', 'tensor'), as said below
- w_value: bfloat16 [2048, 512], P('seq', 'tensor'), may hold values from -0.125 to 0.125
- w_out: bfloat16 [2048, 2048], P('tensor', 'seq'), may hold values from -0.125 to 0.125
- mlp_gain: float32 [2048], replicated, may hold values from 0.1 to 1.9
- w_gate: bfloat16 [2048, 5632], P('seq', 'tensor'), may hold values from -0.125 to 0.125
- w_up: bfloat16 [2048, 5632], P('seq', 'tensor'), may hold values from -0.125 to 0.125
- w_down: bfloat16 [5632, 2048], P('tensor', 'seq'), may hold values from -0.078125 to 0.078125
Outputs:
- layer_out: bfloat16 [32768, 2048], P('seq', 'tensor')
Inputs may be any that keep to these rules, and one draw needn't show every extreme that they name: `w_query`: entries are of order 2048 to the power -1/2. `w_key`: entries are of order 2048 to the power -1/2.
All inputs are finite; a program needn't handle non-finite values.
Results may differ from a plain program's by a relative error of at most 0.013.
Values may be sent and summed in bfloat16 or wider, within the bound.
No kernel may reach another device: no remote copies, remote signals or barrier semaphores. Data moves between devices by JAX's collectives and lax.ppermute only.
A program may use at most 128 MiB of HBM per device.

v0:
```python
import jax
import jax.numpy as jnp
from jax import lax
from jax.sharding import Mesh
from jax.sharding import PartitionSpec as P

HEAD_DIM = 128
WINDOW = 1024
SEQ = ("seq_0", "seq_1", "seq_2")


def copy_for_each(value, axis):
    length = lax.axis_size(axis)
    return lax.all_to_all(
        jnp.broadcast_to(value[None], (length, *value.shape)), axis, 0, 0, tiled=True
    )


def in_order(tiles, dim):
    tiles = jnp.moveaxis(tiles, 0, dim)
    shape = tiles.shape
    return tiles.reshape(*shape[:dim], shape[dim] * shape[dim + 1], *shape[dim + 2 :])


def gathered_copies(value, axis, dim):
    tiles = copy_for_each(value, axis)
    return in_order(tiles, dim)


def sent_together(arrays, axis, dim, along):
    ends, at = ([], 0)
    for a in arrays[:-1]:
        at += a.shape[along]
        ends.append(at)
    both = jnp.concatenate(arrays, axis=along)
    return tuple(jnp.split(lax.all_gather(both, axis, axis=dim, tiled=True), ends, axis=along))


def passed_along(block, axis, distance):
    devices = range(lax.axis_size(axis))
    route = [(i - distance, i) for i in devices if i - distance in devices]
    return lax.ppermute(block, axis, route)


def in_blocks(value, dim, length):
    shape = value.shape
    tiles = value.reshape(*shape[:dim], length, shape[dim] // length, *shape[dim + 1 :])
    return jnp.moveaxis(tiles, dim, 0)


def sent_and_summed(value, axis, dim):
    length = lax.axis_size(axis)
    tiles = lax.all_to_all(in_blocks(value, dim, length), axis, 0, 0, tiled=True)
    return jnp.sum(tiles.astype(jnp.float32), axis=0)


def all_blocks(value, axes, sequence):
    tiles = value[None]
    for k in sequence:
        tiles = lax.all_gather(tiles, axes[k], axis=0, tiled=True)
    carried = [lax.axis_size(axes[k]) for k in reversed(sequence)]
    tiles = tiles.reshape(*carried, *value.shape)
    turned = sorted(range(len(sequence)), key=lambda place: sequence[len(sequence) - 1 - place])
    return tiles.transpose(*turned, *range(len(sequence), tiles.ndim)).reshape(-1, *value.shape)


def gather_axes(value, axes, sequence, dim):
    return in_order(all_blocks(value, axes, sequence), dim)


def scaled_rows(values, gain):
    values = values.astype(jnp.float32)
    mean_square = jnp.mean(values * values, axis=1, keepdims=True)
    return (values * lax.rsqrt(mean_square + 1e-06) * gain).astype(jnp.bfloat16)


def product(left, right):
    return jnp.dot(left, right, preferred_element_type=jnp.float32)


def window_attention(queries, context_keys, context_values, reach, position):
    rows = queries.shape[0]
    local_kv = context_keys.shape[1] // HEAD_DIM
    group = queries.shape[1] // (local_kv * HEAD_DIM)
    block = min(512, rows)
    span = WINDOW + block
    scale = HEAD_DIM ** (-0.5)
    start = reach * rows - WINDOW
    query_block = queries.reshape(block, local_kv, group, HEAD_DIM)
    key_block = context_keys.reshape(span, local_kv, HEAD_DIM)
    value_block = context_values.reshape(span, local_kv, HEAD_DIM)
    scores = (
        jnp.einsum("qkgd,ckd->kgqc", query_block, key_block, preferred_element_type=jnp.float32)
        * scale
    )
    query_pos = lax.broadcasted_iota(jnp.int32, (block, span), 0)
    key_pos = lax.broadcasted_iota(jnp.int32, (block, span), 1)
    distance = query_pos + WINDOW - key_pos
    first_key = (position - reach) * rows + start
    allowed = (distance >= 0) & (distance < WINDOW) & (key_pos + first_key >= 0)
    scores = jnp.where(allowed[None, None], scores, -1e30)
    highest = jnp.max(scores, axis=3, keepdims=True)
    raised = jnp.exp(scores - highest)
    weights = (raised / jnp.sum(raised, axis=3, keepdims=True)).astype(jnp.bfloat16)
    mixed = jnp.einsum("kgqc,ckd->qkgd", weights, value_block, preferred_element_type=jnp.float32)
    outputs = mixed.astype(jnp.bfloat16).reshape(block, local_kv * group * HEAD_DIM)
    return outputs


def per_device(tokens, attn_gain, w_query, w_key, w_value, w_out, mlp_gain, w_gate, w_up, w_down):
    rows = tokens.shape[0]
    whole = gathered_copies(tokens, "tensor", 1)
    normed = scaled_rows(whole, attn_gain)
    query_full, key_full, value_full = sent_together((w_query, w_key, w_value), SEQ, 0, 1)
    queries = product(normed, query_full).astype(jnp.bfloat16)
    keys = product(normed, key_full).astype(jnp.bfloat16)
    values = product(normed, value_full).astype(jnp.bfloat16)
    reach = -(-WINDOW // rows)
    earlier = []
    current = (keys, values)
    for step in range(reach):
        current = passed_along((current[0], current[1]), SEQ, 1)
        earlier.append(current)
    context_keys = jnp.concatenate(
        [earlier[reach - 1 - step][0] for step in range(reach)] + [keys], axis=0
    )
    context_values = jnp.concatenate(
        [earlier[reach - 1 - step][1] for step in range(reach)] + [values], axis=0
    )
    position = lax.axis_index(SEQ)
    attended = window_attention(queries, context_keys, context_values, reach, position)
    out_full = gathered_copies(w_out, SEQ, 1)
    head_terms = product(attended, out_full)
    attn_share = sent_and_summed(head_terms.astype(jnp.bfloat16), "tensor", 1)
    stream_share = (tokens.astype(jnp.float32) + attn_share).astype(jnp.bfloat16)
    stream_whole = gathered_copies(stream_share, "tensor", 1)
    stream_normed = scaled_rows(stream_whole, mlp_gain)
    gate_full, up_full = sent_together((w_gate, w_up), SEQ, 0, 1)
    gate = product(stream_normed, gate_full)
    upward = product(stream_normed, up_full)
    hidden = (jax.nn.silu(gate) * upward).astype(jnp.bfloat16)
    down_full = gather_axes(w_down, SEQ, (0, 1, 2), 1)
    unit_terms = product(hidden, down_full)
    mlp_share = sent_and_summed(unit_terms.astype(jnp.bfloat16), "tensor", 1)
    return (stream_share.astype(jnp.float32) + mlp_share).astype(jnp.bfloat16)


def solution(mesh):
    split = Mesh(
        mesh.devices.reshape(2, 4, 8, mesh.shape["tensor"]), ("seq_0", "seq_1", "seq_2", "tensor")
    )
    placed = (
        P(SEQ, "tensor"),
        P(),
        P(SEQ, "tensor"),
        P(SEQ, "tensor"),
        P(SEQ, "tensor"),
        P("tensor", SEQ),
        P(),
        P(SEQ, "tensor"),
        P(SEQ, "tensor"),
        P("tensor", SEQ),
    )
    return jax.shard_map(
        per_device, mesh=split, in_specs=placed, out_specs=P(SEQ, "tensor"), check_vma=False
    )
```

profile of v0, /device:TPU:1, one launch (start us, length us, event | category | flops | bytes accessed | tf_op | source)
XLA Modules:
  0.0 769.3 jit_solution(572772055486221659)
XLA Ops:
  6.5 1.5 pad_maximum_fusion.1
  8.1 5.0 all-gather
  13.1 13.0 %all_gather.18 = bf16[8,1408,32]{1,2,0:T(8,128)(2,1)} all-gather(bf16[2,1408,32]{1,2,0:T(8,128)(2,1)S(1)} %bitcast.99), channel_id=1, replica_groups=mesh['seq_0'=2,'seq_1'=4,'seq_2'=8,'tensor'=4] {'seq_1'}, dimensions={0}, use_global_device_ids=true | all-gather | bytes 901120 | tf_op jit(solution)/shard_map/all_gather | solution.py:60
  26.1 1.6 pad_maximum_fusion
  28.0 1.5 broadcast_in_dim.20
  29.5 9.4 %all-to-all-start = ((bf16[4,512,512]{1,2,0:T(8,128)(2,1)}), bf16[4,512,512]{1,2,0:T(8,128)(2,1)S(1)}, u32[]{:S(2)}, u32[]{:S(2)}) async-start(bf16[4,512,512]{1,2,0:T(8,128)(2,1)} %broadcast_in_dim.20), calls=%async_computation | async-start | bytes 4194304 | tf_op jit(solution)/shard_map/all_to_all | solution.py:14
  38.9 1.3 fusion.18
  40.2 28.7 %all-to-all-done = bf16[4,512,512]{1,2,0:T(8,128)(2,1)S(1)} async-done(((bf16[4,512,512]{1,2,0:T(8,128)(2,1)}), bf16[4,512,512]{1,2,0:T(8,128)(2,1)S(1)}, u32[]{:S(2)}, u32[]{:S(2)}) %all-to-all-start) | async-done | bytes 2097184 | tf_op jit(solution)/shard_map/all_to_all | solution.py:14
  69.0 1.6 broadcast_in_dim.23
  70.5 9.6 %all-to-all-start.1 = ((bf16[64,512,32]{1,2,0:T(8,128)(2,1)}), bf16[64,512,32]{1,2,0:T(8,128)(2,1)}, u32[]{:S(2)}, u32[]{:S(2)}) async-start(bf16[64,512,32]{1,2,0:T(8,128)(2,1)} %broadcast_in_dim.23), calls=%async_computation.1 | async-start | bytes 4194304 | tf_op jit(solution)/shard_map/all_to_all | solution.py:14
  80.6 1.9 fusion.11
  82.6 194.5 %all-gather.5.cloned.1.call-done = bf16[2048,768]{1,0:T(8,128)(2,1)} async-done(((bf16[32,768]{1,0:T(8,128)(2,1)}), bf16[2048,768]{1,0:T(8,128)(2,1)}) %all-gather.5.cloned.1.call-update) | async-done | bytes 3145744 | tf_op jit(solution)/shard_map/all_gather | solution.py:36
  277.0 2.6 convolution_convert_fusion.2
  279.6 1.3 collective-permute-start.2
  280.9 2.4 convolution_convert_fusion.3
  283.4 1.8 collective-permute-start
  285.2 1.9 collective-permute-start.3
  287.2 1.3 fusion.24
  288.5 3.1 collective-permute-start.1
  291.6 2.4 fusion.1
  294.0 2.8 fusion
  296.8 4.1 fusion.27
  300.8 2.9 convolution_convert_fusion
  303.9 79.6 %all_to_all.25 = bf16[4,512,512]{2,1,0:T(8,128)(2,1)S(1)} all-to-all(bf16[4,512,512]{2,1,0:T(8,128)(2,1)S(1)} %bitcast.93), channel_id=1, replica_groups=mesh['seq_0'=2,'seq_1'=4,'seq_2'=8,'tensor'=4] {'tensor'}, dimensions={0} | all-to-all | bytes 4194304 | tf_op jit(solution)/shard_map/all_to_all | solution.py:53
  384.4 34.1 %all_to_all.26 = bf16[4,512,512]{1,2,0:T(8,128)(2,1)S(1)} all-to-all(bf16[4,512,512]{1,2,0:T(8,128)(2,1)S(1)} %broadcast_in_dim.24), channel_id=1, replica_groups=mesh['seq_0'=2,'seq_1'=4,'seq_2'=8,'tensor'=4] {'tensor'}, dimensions={0} | all-to-all | bytes 4194304 | tf_op jit(solution)/shard_map/all_to_all | solution.py:14
  419.0 0.5 fusion.9
  419.6 6.5 copy.49
  426.1 241.3 %all-gather.7.cloned.1.call-done = bf16[2048,2816]{1,0:T(8,128)(2,1)} async-done(((bf16[32,2816]{1,0:T(8,128)(2,1)}), bf16[2048,2816]{1,0:T(8,128)(2,1)}) %all-gather.7.cloned.1.call-update) | async-done | bytes 11534352 | tf_op jit(solution)/shard_map/all_gather | solution.py:36
  667.5 7.7 %fusion.6 = f32[512,1408]{1,0:T(8,128)} fusion(bf16[512,2048]{0,1:T(8,128)(2,1)S(1)} %fusion.9, bf16[2048,2816]{1,0:T(8,128)(2,1)} %all-gather.7.cloned.1.call-done), kind=kOutput, calls=%fused_computation.9 | convolution fusion | flops 2952790016 | bytes 10747904 | tf_op jit(solution)/shard_map/dot_general | solution.py:78
  675.2 12.8 %convolution_convert_fusion.1 = bf16[512,2048]{1,0:T(8,128)(2,1)S(1)} fusion(bf16[1408,2048]{0,1:T(8,128)(2,1)} %bitcast.96, bf16[512,2048]{0,1:T(8,128)(2,1)} %copy-done.1, bf16[2048,2816]{1,0:T(8,128)(2,1)} %all-gather.7.cloned.1.call-done, f32[512,1408]{1,0:T(8,128)} %fusion.6), kind=kOutput, calls=%fused_computation.29 | convolution fusion | flops 5910953984 | bytes 18612224 | tf_op jit(solution)/shard_map/dot_general | solution.py:78
  688.2 73.2 %all_to_all.27 = bf16[4,512,512]{2,1,0:T(8,128)(2,1)S(1)} all-to-all(bf16[4,512,512]{2,1,0:T(8,128)(2,1)S(1)} %bitcast.94), channel_id=1, replica_groups=mesh['seq_0'=2,'seq_1'=4,'seq_2'=8,'tensor'=4] {'tensor'}, dimensions={0} | all-to-all | bytes 4194304 | tf_op jit(solution)/shard_map/all_to_all | solution.py:53
  761.8 1.0 add_convert_fusion
  (41 shorter events, 3.0 us)
Async XLA Ops:
  6.5 21.2 %copy-start.2 = (bf16[512,512]{1,0:T(8,128)(2,1)S(1)}, bf16[512,512]{1,0:T(8,128)(2,1)}, u32[]{:S(2)}) copy-start(bf16[512,512]{1,0:T(8,128)(2,1)} %param.10) | copy-start | bytes 1572868
  6.5 270.5 %all-gather.5.cloned.1.call-start = ((), (), s32[]{:S(2)}) async-start(), calls=%async_computation.5 | async-start | bytes 3194880 | tf_op jit(solution)/shard_map/all_gather | solution.py:36
  8.0 411.6 %all-gather.9.cloned.1.call-start = ((), (), s32[]{:S(2)}) async-start(), calls=%async_computation.7 | async-start | bytes 6488064 | tf_op jit(solution)/shard_map/all_gather | solution.py:60
  26.1 641.4 %all-gather.7.cloned.1.call-start = ((), (), s32[]{:S(2)}) async-start(), calls=%async_computation.6 | async-start | bytes 11714560 | tf_op jit(solution)/shard_map/all_gather | solution.py:36
  29.5 39.5 %copy-start.3 = (bf16[512,32]{0,1:T(8,128)(2,1)S(1)}, bf16[512,32]{0,1:T(8,128)(2,1)}, u32[]{:S(2)}) copy-start(bf16[512,32]{0,1:T(8,128)(2,1)} %param.15) | copy-start | bytes 98308
  29.5 39.5 %all-to-all-start = ((bf16[4,512,512]{1,2,0:T(8,128)(2,1)}), bf16[4,512,512]{1,2,0:T(8,128)(2,1)S(1)}, u32[]{:S(2)}, u32[]{:S(2)}) async-start(bf16[4,512,512]{1,2,0:T(8,128)(2,1)} %broadcast_in_dim.20), calls=%async_computation | async-start | bytes 4194304 | tf_op jit(solution)/shard_map/all_to_all | solution.py:14
  70.5 10.1 %copy-start.4 = (f32[2048]{0:T(1024)S(1)}, f32[2048]{0:T(1024)}, u32[]{:S(2)}) copy-start(f32[2048]{0:T(1024)} %param.11) | copy-start | bytes 24580
  70.5 230.3 %all-to-all-start.1 = ((bf16[64,512,32]{1,2,0:T(8,128)(2,1)}), bf16[64,512,32]{1,2,0:T(8,128)(2,1)}, u32[]{:S(2)}, u32[]{:S(2)}) async-start(bf16[64,512,32]{1,2,0:T(8,128)(2,1)} %broadcast_in_dim.23), calls=%async_computation.1 | async-start | bytes 4194304 | tf_op jit(solution)/shard_map/all_to_all | solution.py:14
  82.6 204.6 %copy-start = (bf16[512,2048]{0,1:T(8,128)(2,1)S(1)}, bf16[512,2048]{0,1:T(8,128)(2,1)}, u32[]{:S(2)}) copy-start(bf16[512,2048]{0,1:T(8,128)(2,1)} %fusion.11) | copy-start | bytes 6291460
  277.0 10.1 %copy-start.6 = (bf16[2048,768]{1,0:T(8,128)(2,1)S(1)}, bf16[2048,768]{1,0:T(8,128)(2,1)}, u32[]{:S(2)}) copy-start(bf16[2048,768]{1,0:T(8,128)(2,1)} %all-gather.5.cloned.1.call-done) | copy-start | bytes 9437188
  279.6 5.6 collective-permute-start.2
  283.4 5.1 collective-permute-start
  285.2 6.4 collective-permute-start.3
  288.5 8.3 %collective-permute-start.1 = (bf16[512,128]{1,0:T(8,128)(2,1)S(1)}, bf16[512,128]{1,0:T(8,128)(2,1)S(1)}, u32[]{:S(2)}, u32[]{:S(2)}) collective-permute-start(bf16[512,128]{1,0:T(8,128)(2,1)S(1)} %collective-permute-done), channel_id=1, source_target_pairs={{0,4},{4,8},{8,12},{12,16},{16,20},{20,24},{24,28},{28,32},{32,36}... | collective-permute-start | bytes 393224 | tf_op jit(solution)/shard_map/ppermute | solution.py:42
  384.4 34.6 %copy-start.5 = (f32[2048]{0:T(1024)S(1)}, f32[2048]{0:T(1024)}, u32[]{:S(2)}) copy-start(f32[2048]{0:T(1024)} %param.16) | copy-start | bytes 24580
  419.6 247.9 %copy-start.1 = (bf16[512,2048]{0,1:T(8,128)(2,1)}, bf16[512,2048]{0,1:T(8,128)(2,1)S(1)}, u32[]{:S(2)}) copy-start(bf16[512,2048]{0,1:T(8,128)(2,1)S(1)} %fusion.9) | copy-start | bytes 6291460
Sparse Core Ops, SparseCore 0:
  9.1 267.8 all-gather.4
  278.8 110.4 all-gather.8
  391.1 276.3 all-gather.6
where the time goes:
time: 770 us; the launch traced here: 769 us
  waiting for transfers between devices  465 us (60%)
  blocking collectives  205 us (27%)
  matrix products  36.2 us (5%)
  starting transfers between devices  27.3 us (4%)
  between operations  13.4 us (2%)
  other arithmetic  12.4 us (2%)
  local copies, waits for them, and re-layouts  10.6 us (1%)
    all_gather x2, waiting for transfers between devices, sent_together(): lax.all_gather(both, axis, axis=dim, tiled=True)  436 us
    all_to_all x2, blocking collectives, sent_and_summed(): lax.all_to_all(in_blocks(value, dim, length), axis, 0, 0, tiled=True)  153 us
    all_to_all x1, blocking collectives, copy_for_each(): lax.all_to_all(jnp.broadcast_to(value[None], (length, *value.shape)), axi...  34.1 us
    dot_general x6, matrix products, product(): return jnp.dot(left, right, preferred_element_type=jnp.float32)  29.8 us
    all_to_all x2, waiting for transfers between devices, copy_for_each(): lax.all_to_all(jnp.broadcast_to(value[None], (length, *value.shape)), axi...  28.7 us
    all_to_all x2, starting transfers between devices, copy_for_each(): lax.all_to_all(jnp.broadcast_to(value[None], (length, *value.shape)), axi...  19 us
    all_gather x2, blocking collectives, all_blocks(): tiles = lax.all_gather(tiles, axes[k], axis=0, tiled=True)  17.9 us
  transfers between devices with their start and end apart: 9, of which 3 were waited for; matrix products, arithmetic and copies ran while one was open for 5% of the time, Pallas kernels for 0%

commit v1 on v0

--- a/solution.py
+++ b/solution.py
@@ -57,7 +57,9 @@
 def all_blocks(value, axes, sequence):
     tiles = value[None]
     for k in sequence:
-        tiles = lax.all_gather(tiles, axes[k], axis=0, tiled=True)
+        tiles = jnp.concatenate(
+            lax.all_to_all(jnp.stack([tiles] * lax.axis_size(axes[k])), axes[k], 0, 0), axis=0
+        )
     carried = [lax.axis_size(axes[k]) for k in reversed(sequence)]
     tiles = tiles.reshape(*carried, *value.shape)
     turned = sorted(range(len(sequence)), key=lambda place: sequence[len(sequence) - 1 - place])

time: 770 us -> 763 us (level)
  waiting for transfers between devices: 465 us -> 430 us
  starting transfers between devices: 27.3 us -> 45.1 us
    all_gather x2, waiting for transfers between devices: 436 us -> 218 us  [sent_together(): lax.all_gather(both, axis, axis=dim, tiled=True)]
    all_to_all x0 -> x3, waiting for transfers between devices: none -> 186 us  [all_blocks(): lax.all_to_all(jnp.stack([tiles] * lax.axis_size(axes[k])), axes[k], 0, 0)]
    all_to_all x0 -> x3, starting transfers between devices: none -> 18.4 us  [all_blocks(): lax.all_to_all(jnp.stack([tiles] * lax.axis_size(axes[k])), axes[k], 0, 0)]
    all_gather x2 -> x0, blocking collectives: 17.9 us -> none  [all_blocks(): tiles = lax.all_gather(tiles, axes[k], axis=0, tiled=True)]
    all_to_all x1, blocking collectives: 34.1 us -> 47.4 us  [copy_for_each(): lax.all_to_all(jnp.broadcast_to(value[None], (length, *value.shape)), axi...]
  transfers between devices with their start and end apart: 9 -> 11, of which waited for: 3 -> 6; matrix products, arithmetic and copies ran while one was open for 5% -> 6% of each run, Pallas kernels for 0% -> 0%
where the time goes in v1:
time: 763 us; the launch traced here: 762 us
  waiting for transfers between devices  430 us (56%)
  blocking collectives  206 us (27%)
  starting transfers between devices  45.1 us (6%)
  matrix products  36.1 us (5%)
  local copies, waits for them, and re-layouts  16.3 us (2%)
  other arithmetic  15.4 us (2%)
  between operations  13.6 us (2%)
    all_gather x2, waiting for transfers between devices, sent_together(): lax.all_gather(both, axis, axis=dim, tiled=True)  218 us
    all_to_all x3, waiting for transfers between devices, all_blocks(): lax.all_to_all(jnp.stack([tiles] * lax.axis_size(axes[k])), axes[k], 0, 0)  186 us
    all_to_all x2, blocking collectives, sent_and_summed(): lax.all_to_all(in_blocks(value, dim, length), axis, 0, 0, tiled=True)  159 us
    all_to_all x1, blocking collectives, copy_for_each(): lax.all_to_all(jnp.broadcast_to(value[None], (length, *value.shape)), axi...  47.4 us
    dot_general x6, matrix products, product(): return jnp.dot(left, right, preferred_element_type=jnp.float32)  29.6 us
    all_to_all x2, waiting for transfers between devices, copy_for_each(): lax.all_to_all(jnp.broadcast_to(value[None], (length, *value.shape)), axi...  26.6 us
    all_to_all x3, starting transfers between devices, all_blocks(): lax.all_to_all(jnp.stack([tiles] * lax.axis_size(axes[k])), axes[k], 0, 0)  18.4 us
    all_to_all x2, starting transfers between devices, copy_for_each(): lax.all_to_all(jnp.broadcast_to(value[None], (length, *value.shape)), axi...  17.2 us
  transfers between devices with their start and end apart: 11, of which 6 were waited for; matrix products, arithmetic and copies ran while one was open for 6% of the time, Pallas kernels for 0%

profile of v1, /device:TPU:1, one launch (start us, length us, event | category | flops | bytes accessed | tf_op | source)
XLA Modules:
  0.0 762.3 jit_solution(11427931851733492878)
XLA Ops:
  8.0 1.6 pad_maximum_fusion
  12.4 6.9 all-to-all-start
  21.3 26.6 %all-to-all-done = bf16[4,512,512]{1,2,0:T(8,128)(2,1)S(1)} async-done(((bf16[4,512,512]{1,2,0:T(8,128)(2,1)}), bf16[4,512,512]{1,2,0:T(8,128)(2,1)S(1)}, u32[]{:S(2)}, u32[]{:S(2)}) %all-to-all-start) | async-done | bytes 2097184 | tf_op jit(solution)/shard_map/all_to_all | solution.py:14
  47.9 1.6 broadcast_in_dim.21
  49.5 10.3 %all-to-all-start.1 = ((bf16[64,512,32]{1,2,0:T(8,128)(2,1)}), bf16[64,512,32]{1,2,0:T(8,128)(2,1)}, u32[]{:S(2)}, u32[]{:S(2)}) async-start(bf16[64,512,32]{1,2,0:T(8,128)(2,1)} %broadcast_in_dim.21), calls=%async_computation.1 | async-start | bytes 4194304 | tf_op jit(solution)/shard_map/all_to_all | solution.py:14
  60.3 1.9 fusion.11
  62.2 215.2 %all-gather.3.cloned.1.call-done = bf16[2048,768]{1,0:T(8,128)(2,1)} async-done(((bf16[32,768]{1,0:T(8,128)(2,1)}), bf16[2048,768]{1,0:T(8,128)(2,1)}) %all-gather.3.cloned.1.call-update) | async-done | bytes 3145744 | tf_op jit(solution)/shard_map/all_gather | solution.py:36
  277.4 2.6 convolution_convert_fusion.2
  280.0 2.5 collective-permute-start.2
  282.5 2.4 convolution_convert_fusion.3
  284.9 1.9 collective-permute-start
  286.9 1.9 collective-permute-start.3
  290.1 3.1 collective-permute-start.1
  293.2 2.4 fusion.1
  295.6 2.8 fusion
  298.4 4.1 fusion.27
  302.5 9.8 %all-to-all-start.4 = ((bf16[2,1,1408,32]{2,3,1,0:T(8,128)(2,1)}), bf16[2,1,1408,32]{2,3,1,0:T(8,128)(2,1)S(1)}, u32[]{:S(2)}, u32[]{:S(2)}) async-start(bf16[2,1,1408,32]{2,3,1,0:T(8,128)(2,1)} %pad_maximum_fusion.1), calls=%async_computation.4 | async-start | bytes 360448 | tf_op jit(solution)/shard_map/all_to_all | solution.py:61
  312.3 2.9 convolution_convert_fusion
  315.2 1.6 copy.45
  317.0 97.5 %all_to_all.40 = bf16[4,512,512]{2,1,0:T(8,128)(2,1)S(1)} all-to-all(bf16[4,512,512]{2,1,0:T(8,128)(2,1)} %bitcast.92), channel_id=1, replica_groups=mesh['seq_0'=2,'seq_1'=4,'seq_2'=8,'tensor'=4] {'tensor'}, dimensions={0} | all-to-all | bytes 4194304 | tf_op jit(solution)/shard_map/all_to_all | solution.py:53
  415.5 3.5 all-to-all-start.5
  420.7 15.9 %all-to-all-done.5 = bf16[4,2,1408,32]{2,3,1,0:T(8,128)(2,1)S(1)} async-done(((bf16[4,2,1408,32]{2,3,1,0:T(8,128)(2,1)}), bf16[4,2,1408,32]{2,3,1,0:T(8,128)(2,1)S(1)}, u32[]{:S(2)}, u32[]{:S(2)}) %all-to-all-start.5) | async-done | bytes 720928 | tf_op jit(solution)/shard_map/all_to_all | solution.py:61
  436.8 47.4 %all_to_all.41 = bf16[4,512,512]{1,2,0:T(8,128)(2,1)S(1)} all-to-all(bf16[4,512,512]{1,2,0:T(8,128)(2,1)S(1)} %broadcast_in_dim.22), channel_id=1, replica_groups=mesh['seq_0'=2,'seq_1'=4,'seq_2'=8,'tensor'=4] {'tensor'}, dimensions={0} | all-to-all | bytes 4194304 | tf_op jit(solution)/shard_map/all_to_all | solution.py:14
  484.2 3.0 stack.11
  487.2 5.0 all-to-all-start.6
  492.8 1.9 fusion.9
  494.7 169.4 %all-to-all-done.6 = bf16[8,8,1408,32]{2,3,1,0:T(8,128)(2,1)} async-done(((bf16[8,8,1408,32]{2,3,1,0:T(8,128)(2,1)}), bf16[8,8,1408,32]{2,3,1,0:T(8,128)(2,1)}, u32[]{:S(2)}, u32[]{:S(2)}) %all-to-all-start.6) | async-done | bytes 5767200 | tf_op jit(solution)/shard_map/all_to_all | solution.py:61
  664.1 5.9 copy.34
  670.0 2.6 all-gather.5.cloned.1.call-done
  672.5 7.6 %fusion.6 = f32[512,1408]{1,0:T(8,128)} fusion(bf16[512,2048]{0,1:T(8,128)(2,1)S(1)} %copy-done.1, bf16[2048,2816]{1,0:T(8,128)(2,1)} %all-gather.5.cloned.1.call-done), kind=kOutput, calls=%fused_computation.9 | convolution fusion | flops 2952790016 | bytes 10747904 | tf_op jit(solution)/shard_map/dot_general | solution.py:80
  680.2 12.8 %convolution_convert_fusion.1 = bf16[512,2048]{1,0:T(8,128)(2,1)S(1)} fusion(bf16[1408,2048]{0,1:T(8,128)(2,1)} %bitcast.94, bf16[512,2048]{0,1:T(8,128)(2,1)} %fusion.9, bf16[2048,2816]{1,0:T(8,128)(2,1)} %all-gather.5.cloned.1.call-done, f32[512,1408]{1,0:T(8,128)} %fusion.6), kind=kOutput, calls=%fused_computation.29 | convolution fusion | flops 5910953984 | bytes 18612224 | tf_op jit(solution)/shard_map/dot_general | solution.py:80
  693.2 61.0 %all_to_all.42 = bf16[4,512,512]{2,1,0:T(8,128)(2,1)S(1)} all-to-all(bf16[4,512,512]{2,1,0:T(8,128)(2,1)S(1)} %bitcast.93), channel_id=1, replica_groups=mesh['seq_0'=2,'seq_1'=4,'seq_2'=8,'tensor'=4] {'tensor'}, dimensions={0} | all-to-all | bytes 4194304 | tf_op jit(solution)/shard_map/all_to_all | solution.py:53
  (44 shorter events, 13.1 us)
Async XLA Ops:
  6.5 270.8 %all-gather.3.cloned.1.call-start = ((), (), s32[]{:S(2)}) async-start(), calls=%async_computation.8 | async-start | bytes 3194880 | tf_op jit(solution)/shard_map/all_gather | solution.py:36
  8.0 664.6 %all-gather.5.cloned.1.call-start = ((), (), s32[]{:S(2)}) async-start(), calls=%async_computation.9 | async-start | bytes 11714560 | tf_op jit(solution)/shard_map/all_gather | solution.py:36
  10.9 8.4 %copy-start.2 = (bf16[1408,32]{0,1:T(8,128)(2,1)S(1)}, bf16[1408,32]{0,1:T(8,128)(2,1)}, u32[]{:S(2)}) copy-start(bf16[1408,32]{0,1:T(8,128)(2,1)} %param.19) | copy-start | bytes 270340
  12.4 35.5 %copy-start.3 = (bf16[512,32]{0,1:T(8,128)(2,1)S(1)}, bf16[512,32]{0,1:T(8,128)(2,1)}, u32[]{:S(2)}) copy-start(bf16[512,32]{0,1:T(8,128)(2,1)} %param.15) | copy-start | bytes 98308
  12.4 35.5 %all-to-all-start = ((bf16[4,512,512]{1,2,0:T(8,128)(2,1)}), bf16[4,512,512]{1,2,0:T(8,128)(2,1)S(1)}, u32[]{:S(2)}, u32[]{:S(2)}) async-start(bf16[4,512,512]{1,2,0:T(8,128)(2,1)} %broadcast_in_dim.18), calls=%async_computation | async-start | bytes 4194304 | tf_op jit(solution)/shard_map/all_to_all | solution.py:14
  49.5 10.8 %copy-start.4 = (f32[2048]{0:T(1024)S(1)}, f32[2048]{0:T(1024)}, u32[]{:S(2)}) copy-start(f32[2048]{0:T(1024)} %param.11) | copy-start | bytes 24580
  49.5 252.9 %all-to-all-start.1 = ((bf16[64,512,32]{1,2,0:T(8,128)(2,1)}), bf16[64,512,32]{1,2,0:T(8,128)(2,1)}, u32[]{:S(2)}, u32[]{:S(2)}) async-start(bf16[64,512,32]{1,2,0:T(8,128)(2,1)} %broadcast_in_dim.21), calls=%async_computation.1 | async-start | bytes 4194304 | tf_op jit(solution)/shard_map/all_to_all | solution.py:14
  62.2 226.6 %copy-start = (bf16[512,2048]{0,1:T(8,128)(2,1)S(1)}, bf16[512,2048]{0,1:T(8,128)(2,1)}, u32[]{:S(2)}) copy-start(bf16[512,2048]{0,1:T(8,128)(2,1)} %fusion.11) | copy-start | bytes 6291460
  277.4 11.4 %copy-start.6 = (bf16[2048,768]{1,0:T(8,128)(2,1)S(1)}, bf16[2048,768]{1,0:T(8,128)(2,1)}, u32[]{:S(2)}) copy-start(bf16[2048,768]{1,0:T(8,128)(2,1)} %all-gather.3.cloned.1.call-done) | copy-start | bytes 9437188
  280.0 6.9 collective-permute-start.2
  284.9 5.2 collective-permute-start
  286.9 6.4 collective-permute-start.3
  290.1 8.2 %collective-permute-start.1 = (bf16[512,128]{1,0:T(8,128)(2,1)S(1)}, bf16[512,128]{1,0:T(8,128)(2,1)S(1)}, u32[]{:S(2)}, u32[]{:S(2)}) collective-permute-start(bf16[512,128]{1,0:T(8,128)(2,1)S(1)} %collective-permute-done), channel_id=1, source_target_pairs={{0,4},{4,8},{8,12},{12,16},{16,20},{20,24},{24,28},{28,32},{32,36}... | collective-permute-start | bytes 393224 | tf_op jit(solution)/shard_map/ppermute | solution.py:42
  302.5 14.6 %all-to-all-start.4 = ((bf16[2,1,1408,32]{2,3,1,0:T(8,128)(2,1)}), bf16[2,1,1408,32]{2,3,1,0:T(8,128)(2,1)S(1)}, u32[]{:S(2)}, u32[]{:S(2)}) async-start(bf16[2,1,1408,32]{2,3,1,0:T(8,128)(2,1)} %pad_maximum_fusion.1), calls=%async_computation.4 | async-start | bytes 360448 | tf_op jit(solution)/shard_map/all_to_all | solution.py:61
  415.5 21.1 %all-to-all-start.5 = ((bf16[4,2,1408,32]{2,3,1,0:T(8,128)(2,1)}), bf16[4,2,1408,32]{2,3,1,0:T(8,128)(2,1)S(1)}, u32[]{:S(2)}, u32[]{:S(2)}) async-start(bf16[4,2,1408,32]{2,3,1,0:T(8,128)(2,1)} %stack.10), calls=%async_computation.5 | async-start | bytes 1441792 | tf_op jit(solution)/shard_map/all_to_all | solution.py:61
  487.2 5.6 copy-start.5
  487.2 176.9 %all-to-all-start.6 = ((bf16[8,8,1408,32]{2,3,1,0:T(8,128)(2,1)}), bf16[8,8,1408,32]{2,3,1,0:T(8,128)(2,1)}, u32[]{:S(2)}, u32[]{:S(2)}) async-start(bf16[8,8,1408,32]{2,3,1,0:T(8,128)(2,1)} %stack.11), calls=%async_computation.6 | async-start | bytes 11534336 | tf_op jit(solution)/shard_map/all_to_all | solution.py:61
  664.1 8.5 %copy-start.1 = (bf16[512,2048]{0,1:T(8,128)(2,1)S(1)}, bf16[512,2048]{0,1:T(8,128)(2,1)}, u32[]{:S(2)}) copy-start(bf16[512,2048]{0,1:T(8,128)(2,1)} %fusion.9) | copy-start | bytes 6291460
Sparse Core Ops, SparseCore 0:
  9.1 268.2 all-gather.2
  279.2 393.3 all-gather.4
